TPU v7x, 32 devices: a whole 2x2x4 slice. The times are simulated.
32 devices in a mesh: chain: 16 (over z, x, core), tok: 2 (over y).
Axes of the slice: x: 2, y: 2, z: 4, core: 2. Of those that a mesh axis runs over, the one named last changes fastest.
Arguments:
- queries: bfloat16 [65536, 128], P(('chain', 'tok')), may hold values from -6 to 6
- keys: bfloat16 [65536, 128], P(('chain', 'tok')), may hold values from -6 to 6
- values: bfloat16 [65536, 128], P(('chain', 'tok')), may hold values from -6 to 6
Outputs:
- attended: bfloat16 [65536, 128], P(('chain', 'tok'))
All inputs are finite; a program needn't handle non-finite values.
Results may differ from a plain program's by a relative error of at most 0.0058.
Values may be sent and summed in bfloat16 or wider, within the bound.
A program may use at most 64 MiB of HBM per device.

v0:
```python
import functools
import math

import jax
import jax.numpy as jnp
from jax import lax
from jax.experimental import pallas as pl
from jax.experimental.pallas import tpu as pltpu
from jax.sharding import PartitionSpec as P

HD = 64
HEADS = 2
WIDE = HEADS * HD
FAR = HD // 2 + 1
BLOCKS = HD // 4 + 1
MESH = pl.DeviceIdType.MESH
F32, BF16 = jnp.float32, jnp.bfloat16


def layout(n_chain, n_tok):
    inner = 1 << ((n_chain.bit_length() - 1) // 2)
    plane = inner * n_tok
    row_parts = min(8, plane)
    blk_parts = plane // row_parts
    units = -(-BLOCKS // blk_parts)
    count = min(3, units)
    cuts = [-(-units * c // count) for c in range(count + 1)]
    return inner, plane, row_parts, blk_parts, units, cuts


def pairs(low, high):
    return [tuple(range(b, min(b + 2, high))) for b in range(low, high, 2)]


def kernel(n_chain, n_tok, q_ref, k_ref, v_ref, o_ref, xx, zz, vt, qf, acc, tot, got, plane_sum,
           far_got, inc_send, inc, out_t, rs_send, rs_recv, z_send, z_recv, ag_send, ag_recv):
    inner, plane, row_parts, blk_parts, units, cuts = layout(n_chain, n_tok)
    outer = n_chain // inner
    rows = WIDE // row_parts
    tokens = q_ref.shape[0]
    tile = 256 if tokens % 256 == 0 else tokens
    tiles = tokens // tile
    chain, tok = lax.axis_index("chain"), lax.axis_index("tok")
    z, me = chain // inner, (chain % inner) * n_tok + tok
    lane = lax.broadcasted_iota(jnp.int32, (tile, WIDE), 1)
    left = lane < HD

    def in_plane(k):
        peer = (me + k) % plane
        return peer, (z * inner + peer // n_tok, peer % n_tok)

    def along(k):
        return (((z + k) % outer) * inner + chain % inner, tok)

    barrier = pltpu.get_barrier_semaphore()
    for k in range(1, plane):
        pl.semaphore_signal(barrier, inc=1, device_id=in_plane(k)[1], device_id_type=MESH)
    for k in range(1, outer):
        pl.semaphore_signal(barrier, inc=1, device_id=along(k), device_id_type=MESH)

    def prepare(ref):
        @pl.loop(0, tiles)
        def _(t):
            at = pl.ds(pl.multiple_of(t * tile, tile), tile)
            x = ref[at, :].astype(F32)
            other = pltpu.roll(x, HD, 1)
            for h in range(HEADS):
                both = jnp.where(left, x, other) if h == 0 else jnp.where(left, other, x)
                xx[h, at, :] = both
                zz[h, at, :] = jnp.where(left, both, pltpu.roll(both, FAR, 1))

    root2 = math.sqrt(2.0)

    def feats(h, b, at):
        x = xx[h, at, :]
        product = zz[h, at, :] * (x if b == 0 else pltpu.roll(x, b, 1))
        if b == 0:
            scale = jnp.where(left, 1.0, 0.0).astype(F32)
        elif b == 1:
            scale = jnp.where(left, root2, 1.0).astype(F32)
        else:
            scale = jnp.float32(root2)
        return (product * scale).astype(BF16)

    def joined(parts, axis=1):
        return parts[0] if len(parts) == 1 else jnp.concatenate(parts, axis=axis)

    def blocks_of(c):
        return cuts[c] * blk_parts, cuts[c + 1] * blk_parts

    def state(c):
        low, high = blocks_of(c)
        real = min(high, BLOCKS)
        acc[pl.ds(low, high - low)] = jnp.zeros((high - low, WIDE, WIDE), F32)

        @pl.loop(0, tiles)
        def _(t):
            at = pl.ds(pl.multiple_of(t * tile, tile), tile)
            for group in pairs(low, real):
                for h in range(HEADS):
                    part = jnp.dot(vt[pl.ds(h * HD, HD), at],
                                   joined([feats(h, b, at) for b in group]),
                                   preferred_element_type=F32)
                    for i, b in enumerate(group):
                        acc[b, pl.ds(h * HD, HD), :] += part[:, i * WIDE:(i + 1) * WIDE]

        tot[pl.ds(low, high - low)] = acc[pl.ds(low, high - low)].astype(BF16)

    def spot(c, who):
        low, _ = blocks_of(c)
        size = cuts[c + 1] - cuts[c]
        row = pl.multiple_of((who % row_parts) * rows, rows)
        return pl.ds(low + (who // row_parts) * size, size), pl.ds(row, rows)

    def span(c):
        return pl.ds(cuts[c], cuts[c + 1] - cuts[c])

    started = []

    def scatter(c):
        for k in range(1, plane):
            peer, device = in_plane(k)
            blk, row = spot(c, peer)
            copy = pltpu.make_async_remote_copy(
                src_ref=tot.at[blk, row, :], dst_ref=got.at[k, span(c)],
                send_sem=rs_send.at[c, k], recv_sem=rs_recv.at[c, k],
                device_id=device, device_id_type=MESH)
            copy.start()
            started.append(copy)
            rs_copies[c].append(copy)
        blk, row = spot(c, me)
        got[0, span(c)] = tot[blk, row, :]

    def piece(c, source):
        return got[(me + plane - source) % plane, span(c)].astype(F32)

    def spread(c):
        for copy in rs_copies[c]:
            copy.wait_recv()
        total = piece(c, 0)
        for source in range(1, plane):
            total = total + piece(c, source)
        plane_sum[span(c)] = total.astype(BF16)
        for k in range(1, outer):
            copy = pltpu.make_async_remote_copy(
                src_ref=plane_sum.at[span(c)], dst_ref=far_got.at[k, span(c)],
                send_sem=z_send.at[c, k], recv_sem=z_recv.at[c, k],
                device_id=along(k), device_id_type=MESH)
            copy.start()
            started.append(copy)
            z_copies[c].append(copy)

    def gather(c):
        running = jnp.zeros((cuts[c + 1] - cuts[c], rows, WIDE), F32)
        for k in range(1, outer):
            z_copies[c][k - 1].wait_recv()
            running = running + jnp.where(k <= z, far_got[k, span(c)].astype(F32), 0.0)
        for g in range(inner):
            for y in range(n_tok):
                running = running + piece(c, g * n_tok + y)
            inc_send[g, span(c)] = running.astype(BF16)
        blk, row = spot(c, me)
        for k in range(1, plane):
            peer, device = in_plane(k)
            copy = pltpu.make_async_remote_copy(
                src_ref=inc_send.at[peer // n_tok, span(c)], dst_ref=inc.at[blk, row, :],
                send_sem=ag_send.at[c, k], recv_sem=ag_recv.at[c, k],
                device_id=device, device_id_type=MESH)
            copy.start()
            started.append(copy)
            ag_copies[c].append(copy)
        inc[blk, row, :] = inc_send[chain % inner, span(c)]

    def expand_queries(c):
        low, high = blocks_of(c)

        @pl.loop(0, tiles)
        def _(t):
            at = pl.ds(pl.multiple_of(t * tile, tile), tile)
            for b in range(low, min(high, BLOCKS)):
                for h in range(HEADS):
                    qf[h, b, at, :] = feats(h, b, at)

    def read(c, first, last):
        for copy in ag_copies[c]:
            copy.wait_recv()
        low, high = blocks_of(c)
        groups = pairs(low, min(high, BLOCKS))
        count = (chain + 1).astype(F32) * (tokens * n_tok)
        factor = 1.0 / (HD * jnp.sqrt(jnp.full((tile, WIDE), count, F32)))

        @pl.loop(0, tiles)
        def _(t):
            at = pl.ds(pl.multiple_of(t * tile, tile), tile)
            sums = []
            for h in range(HEADS):
                row = pl.ds(h * HD, HD)
                part = None if first else out_t[row, at]
                for group in groups:
                    more = lax.dot_general(
                        joined([inc[b, row, :] for b in group]),
                        joined([qf[h, b, at, :] for b in group]),
                        (((1,), (1,)), ((), ())), preferred_element_type=F32)
                    part = more if part is None else part + more
                if last:
                    sums.append(part)
                else:
                    out_t[row, at] = part
            if last:
                whole = jnp.concatenate(sums, axis=0).T
                o_ref[at, :] = (whole * factor).astype(BF16)

    n = len(cuts) - 1
    rs_copies, z_copies, ag_copies = ([[] for _ in range(n)] for _ in range(3))

    prepare(k_ref)

    @pl.loop(0, tiles)
    def _(t):
        at = pl.ds(pl.multiple_of(t * tile, tile), tile)
        vt[:, at] = v_ref[at, :].astype(F32).T.astype(BF16)

    for c in range(n):
        state(c)
        if c == 0:
            pl.semaphore_wait(barrier, plane - 1 + outer - 1)
        scatter(c)
        if c >= 1:
            spread(c - 1)
    prepare(q_ref)
    for c in range(n):
        expand_queries(c)
        if c == 0:
            spread(n - 1)
        gather(c)
    for c in range(n):
        read(c, c == 0, c == n - 1)
    for copy in started:
        copy.wait_send()


def on_device(n_chain, n_tok, queries, keys, values):
    inner, plane, row_parts, blk_parts, units, cuts = layout(n_chain, n_tok)
    outer, n = n_chain // inner, len(cuts) - 1
    rows, tokens = WIDE // row_parts, queries.shape[0]
    blocks = units * blk_parts
    sems = pltpu.SemaphoreType.DMA
    return pl.pallas_call(
        functools.partial(kernel, n_chain, n_tok),
        out_shape=jax.ShapeDtypeStruct((tokens, WIDE), BF16),
        in_specs=[pl.BlockSpec(memory_space=pltpu.VMEM)] * 3,
        out_specs=pl.BlockSpec(memory_space=pltpu.VMEM),
        scratch_shapes=[
            pltpu.VMEM((HEADS, tokens, WIDE), F32),
            pltpu.VMEM((HEADS, tokens, WIDE), F32),
            pltpu.VMEM((WIDE, tokens), BF16),
            pltpu.VMEM((HEADS, BLOCKS, tokens, WIDE), BF16),
            pltpu.VMEM((blocks, WIDE, WIDE), F32),
            pltpu.VMEM((blocks, WIDE, WIDE), BF16),
            pltpu.VMEM((plane, units, rows, WIDE), BF16),
            pltpu.VMEM((units, rows, WIDE), BF16),
            pltpu.VMEM((max(outer, 1), units, rows, WIDE), BF16),
            pltpu.VMEM((inner, units, rows, WIDE), BF16),
            pltpu.VMEM((blocks, WIDE, WIDE), BF16),
            pltpu.VMEM((WIDE, tokens), F32),
            sems((n, plane)), sems((n, plane)),
            sems((n, max(outer, 1))), sems((n, max(outer, 1))),
            sems((n, plane)), sems((n, plane)),
        ],
        compiler_params=pltpu.CompilerParams(
            collective_id=0, has_side_effects=True, vmem_limit_bytes=60 * 1024 * 1024),
    )(queries, keys, values)


def solution(mesh):
    placed = P(("chain", "tok"), None)
    return jax.shard_map(
        functools.partial(on_device, mesh.shape["chain"], mesh.shape["tok"]),
        mesh=mesh, in_specs=(placed,) * 3, out_specs=placed, check_vma=False)
```

profile of v0, /device:TPU:0, one launch (start us, length us, event | category | flops | bytes accessed | tf_op | source)
XLA Modules:
  0.0 44.4 jit_solution(10929124476003368368)
XLA Ops:
  0.0 42.5 %shard_map.37 = bf16[2048,128]{1,0:T(8,128)(2,1)} custom-call(bf16[2048,128]{1,0:T(8,128)(2,1)} %q_ref.1, bf16[2048,128]{1,0:T(8,128)(2,1)} %k_ref.1, bf16[2048,128]{1,0:T(8,128)(2,1)} %v_ref.1), custom_call_target="tpu_custom_call" | custom-call | tf_op jit(solution)/shard_map/pallas_call | solution.py:248
  42.5 1.9 %copy.5 = bf16[2048,128]{1,0:T(8,128)(2,1)} copy(bf16[2048,128]{1,0:T(8,128)(2,1)} %shard_map.37) | data formatting | bytes 1048576
where the time goes:
time: 44.7 us; the launch traced here: 44.4 us
  Pallas kernels  42.5 us (95%)
  local copies, waits for them, and re-layouts  1.87 us (4%)
    pallas_call x1, Pallas kernels, on_device(): pl.pallas_call(functools.partial(kernel, n_chain, n_tok), out_shape=jax.S...  42.5 us
    unnamed x1, local copies, waits for them, and re-layouts  1.87 us

commit v1 on v0

--- a/solution.py
+++ b/solution.py
@@ -11,8 +11,9 @@
 HD = 64
 HEADS = 2
 WIDE = HEADS * HD
-FAR = HD // 2 + 1
+HALF = HD // 2
 BLOCKS = HD // 4 + 1
+LANES, DEEP = 128, 256
 MESH = pl.DeviceIdType.MESH
 F32, BF16 = jnp.float32, jnp.bfloat16
 
@@ -32,18 +33,15 @@
     return [tuple(range(b, min(b + 2, high))) for b in range(low, high, 2)]
 
 
-def kernel(n_chain, n_tok, q_ref, k_ref, v_ref, o_ref, xx, zz, vt, qf, acc, tot, got, plane_sum,
+def kernel(n_chain, n_tok, q_ref, k_ref, v_ref, o_ref, xs, zs, qf, tot, got, plane_sum,
            far_got, inc_send, inc, out_t, rs_send, rs_recv, z_send, z_recv, ag_send, ag_recv):
     inner, plane, row_parts, blk_parts, units, cuts = layout(n_chain, n_tok)
     outer = n_chain // inner
     rows = WIDE // row_parts
     tokens = q_ref.shape[0]
-    tile = 256 if tokens % 256 == 0 else tokens
-    tiles = tokens // tile
+    tiles = tokens // LANES
     chain, tok = lax.axis_index("chain"), lax.axis_index("tok")
     z, me = chain // inner, (chain % inner) * n_tok + tok
-    lane = lax.broadcasted_iota(jnp.int32, (tile, WIDE), 1)
-    left = lane < HD
 
     def in_plane(k):
         peer = (me + k) % plane
@@ -58,32 +56,34 @@
     for k in range(1, outer):
         pl.semaphore_signal(barrier, inc=1, device_id=along(k), device_id_type=MESH)
 
+    root2 = math.sqrt(2.0)
+
     def prepare(ref):
         @pl.loop(0, tiles)
         def _(t):
-            at = pl.ds(pl.multiple_of(t * tile, tile), tile)
-            x = ref[at, :].astype(F32)
-            other = pltpu.roll(x, HD, 1)
+            x = ref[pl.ds(pl.multiple_of(t * LANES, LANES), LANES), :].astype(F32).T
             for h in range(HEADS):
-                both = jnp.where(left, x, other) if h == 0 else jnp.where(left, other, x)
-                xx[h, at, :] = both
-                zz[h, at, :] = jnp.where(left, both, pltpu.roll(both, FAR, 1))
-
-    root2 = math.sqrt(2.0)
-
-    def feats(h, b, at):
-        x = xx[h, at, :]
-        product = zz[h, at, :] * (x if b == 0 else pltpu.roll(x, b, 1))
-        if b == 0:
-            scale = jnp.where(left, 1.0, 0.0).astype(F32)
-        elif b == 1:
-            scale = jnp.where(left, root2, 1.0).astype(F32)
+                own = x[h * HD:(h + 1) * HD]
+                xs[h, t] = own
+                wide = own * root2
+                zs[h, t, pl.ds(0, HD), :] = wide
+                zs[h, t, pl.ds(HD, HALF), :] = wide[:HALF]
+
+    def feats(h, t, d):
+        x = xs[h, t]
+        if d == 0:
+            other = x
+        elif d == HALF:
+            other = jnp.concatenate([x[HALF:], x[:HALF]], axis=0)
         else:
-            scale = jnp.float32(root2)
-        return (product * scale).astype(BF16)
+            other = zs[h, t, pl.ds(d, HD), :]
+        return (x * other).astype(BF16)
 
     def joined(parts, axis=1):
         return parts[0] if len(parts) == 1 else jnp.concatenate(parts, axis=axis)
+
+    def dists(b):
+        return [d for d in (2 * b, 2 * b + 1) if d <= HALF]
 
     def blocks_of(c):
         return cuts[c] * blk_parts, cuts[c + 1] * blk_parts
@@ -91,20 +91,27 @@
     def state(c):
         low, high = blocks_of(c)
         real = min(high, BLOCKS)
-        acc[pl.ds(low, high - low)] = jnp.zeros((high - low, WIDE, WIDE), F32)
-
-        @pl.loop(0, tiles)
-        def _(t):
-            at = pl.ds(pl.multiple_of(t * tile, tile), tile)
-            for group in pairs(low, real):
-                for h in range(HEADS):
-                    part = jnp.dot(vt[pl.ds(h * HD, HD), at],
-                                   joined([feats(h, b, at) for b in group]),
-                                   preferred_element_type=F32)
-                    for i, b in enumerate(group):
-                        acc[b, pl.ds(h * HD, HD), :] += part[:, i * WIDE:(i + 1) * WIDE]
-
-        tot[pl.ds(low, high - low)] = acc[pl.ds(low, high - low)].astype(BF16)
+        for group in pairs(low, real):
+            ds = [d for b in group for d in dists(b)]
+            parts = []
+            for h in range(HEADS):
+                part = None
+                for k in range(tokens // DEEP):
+                    lhs = joined([joined([feats(h, t, d) for d in ds], axis=0)
+                                  for t in range(k * DEEP // LANES, (k + 1) * DEEP // LANES)])
+                    more = jnp.dot(lhs, v_ref[pl.ds(k * DEEP, DEEP), :], preferred_element_type=F32)
+                    part = more if part is None else part + more
+                parts.append(part)
+            left = lax.broadcasted_iota(jnp.int32, parts[0].shape, 1) < HD
+            both = jnp.where(left, parts[0], parts[1])
+            short = len(group) * WIDE - both.shape[0]
+            if short:
+                both = jnp.concatenate([both, jnp.zeros((short, WIDE), F32)], axis=0)
+            for i, b in enumerate(group):
+                tot[b] = both[i * WIDE:(i + 1) * WIDE].T.astype(BF16)
+        if high > max(low, real):
+            first = max(low, real)
+            tot[pl.ds(first, high - first)] = jnp.zeros((high - first, WIDE, WIDE), BF16)
 
     def spot(c, who):
         low, _ = blocks_of(c)
@@ -176,10 +183,11 @@
 
         @pl.loop(0, tiles)
         def _(t):
-            at = pl.ds(pl.multiple_of(t * tile, tile), tile)
+            at = pl.ds(pl.multiple_of(t * LANES, LANES), LANES)
             for b in range(low, min(high, BLOCKS)):
-                for h in range(HEADS):
-                    qf[h, b, at, :] = feats(h, b, at)
+                for d in dists(b):
+                    for h in range(HEADS):
+                        qf[h, pl.ds(d * HD, HD), at] = feats(h, t, d)
 
     def read(c, first, last):
         for copy in ag_copies[c]:
@@ -187,38 +195,33 @@
         low, high = blocks_of(c)
         groups = pairs(low, min(high, BLOCKS))
         count = (chain + 1).astype(F32) * (tokens * n_tok)
-        factor = 1.0 / (HD * jnp.sqrt(jnp.full((tile, WIDE), count, F32)))
-
-        @pl.loop(0, tiles)
-        def _(t):
-            at = pl.ds(pl.multiple_of(t * tile, tile), tile)
+        factor = 1.0 / (HD * jnp.sqrt(jnp.full((LANES, WIDE), count, F32)))
+        for k in range(tokens // DEEP):
+            at = pl.ds(k * DEEP, DEEP)
             sums = []
             for h in range(HEADS):
                 row = pl.ds(h * HD, HD)
                 part = None if first else out_t[row, at]
                 for group in groups:
-                    more = lax.dot_general(
-                        joined([inc[b, row, :] for b in group]),
-                        joined([qf[h, b, at, :] for b in group]),
-                        (((1,), (1,)), ((), ())), preferred_element_type=F32)
+                    depth = sum(len(dists(b)) for b in group) * HD
+                    state_t = joined([inc[b, row, :] for b in group])[:, :depth]
+                    more = jnp.dot(state_t, qf[h, pl.ds(group[0] * WIDE, depth), at],
+                                   preferred_element_type=F32)
                     part = more if part is None else part + more
                 if last:
                     sums.append(part)
                 else:
                     out_t[row, at] = part
             if last:
-                whole = jnp.concatenate(sums, axis=0).T
-                o_ref[at, :] = (whole * factor).astype(BF16)
+                whole = jnp.concatenate(sums, axis=0)
+                for i in range(DEEP // LANES):
+                    o_ref[pl.ds(k * DEEP + i * LANES, LANES), :] = (
+                        whole[:, i * LANES:(i + 1) * LANES].T * factor).astype(BF16)
 
     n = len(cuts) - 1
     rs_copies, z_copies, ag_copies = ([[] for _ in range(n)] for _ in range(3))
 
     prepare(k_ref)
-
-    @pl.loop(0, tiles)
-    def _(t):
-        at = pl.ds(pl.multiple_of(t * tile, tile), tile)
-        vt[:, at] = v_ref[at, :].astype(F32).T.astype(BF16)
 
     for c in range(n):
         state(c)
@@ -251,11 +254,9 @@
         in_specs=[pl.BlockSpec(memory_space=pltpu.VMEM)] * 3,
         out_specs=pl.BlockSpec(memory_space=pltpu.VMEM),
         scratch_shapes=[
-            pltpu.VMEM((HEADS, tokens, WIDE), F32),
-            pltpu.VMEM((HEADS, tokens, WIDE), F32),
-            pltpu.VMEM((WIDE, tokens), BF16),
-            pltpu.VMEM((HEADS, BLOCKS, tokens, WIDE), BF16),
-            pltpu.VMEM((blocks, WIDE, WIDE), F32),
+            pltpu.VMEM((HEADS, tokens // LANES, HD, LANES), F32),
+            pltpu.VMEM((HEADS, tokens // LANES, HD + HALF, LANES), F32),
+            pltpu.VMEM((HEADS, BLOCKS * WIDE, tokens), BF16),
             pltpu.VMEM((blocks, WIDE, WIDE), BF16),
             pltpu.VMEM((plane, units, rows, WIDE), BF16),
             pltpu.VMEM((units, rows, WIDE), BF16),

time: 44.7 us -> 30.4 us (0.68)
  Pallas kernels: 42.5 us -> 28.4 us
    pallas_call x1, Pallas kernels: 42.5 us -> 28.4 us  [on_device(): pl.pallas_call(functools.partial(kernel, n_chain, n_tok), out_shape=jax.S...]
where the time goes in v1:
time: 30.4 us; the launch traced here: 30.2 us
  Pallas kernels  28.4 us (93%)
  local copies, waits for them, and re-layouts  1.87 us (6%)
    pallas_call x1, Pallas kernels, on_device(): pl.pallas_call(functools.partial(kernel, n_chain, n_tok), out_shape=jax.S...  28.4 us
    unnamed x1, local copies, waits for them, and re-layouts  1.87 us

profile of v1, /device:TPU:0, one launch (start us, length us, event | category | flops | bytes accessed | tf_op | source)
XLA Modules:
  0.0 30.2 jit_solution(8523248097726835023)
XLA Ops:
  0.0 28.4 %shard_map.37 = bf16[2048,128]{1,0:T(8,128)(2,1)} custom-call(bf16[2048,128]{1,0:T(8,128)(2,1)} %q_ref.1, bf16[2048,128]{1,0:T(8,128)(2,1)} %k_ref.1, bf16[2048,128]{1,0:T(8,128)(2,1)} %v_ref.1), custom_call_target="tpu_custom_call" | custom-call | tf_op jit(solution)/shard_map/pallas_call | solution.py:251
  28.4 1.9 %copy.5 = bf16[2048,128]{1,0:T(8,128)(2,1)} copy(bf16[2048,128]{1,0:T(8,128)(2,1)} %shard_map.37) | data formatting | bytes 1048576

commit v2 on v1

--- a/solution.py
+++ b/solution.py
@@ -14,6 +14,7 @@
 HALF = HD // 2
 BLOCKS = HD // 4 + 1
 LANES, DEEP = 128, 256
+CHUNKS = 4
 MESH = pl.DeviceIdType.MESH
 F32, BF16 = jnp.float32, jnp.bfloat16
 
@@ -24,8 +25,9 @@
     row_parts = min(8, plane)
     blk_parts = plane // row_parts
     units = -(-BLOCKS // blk_parts)
-    count = min(3, units)
-    cuts = [-(-units * c // count) for c in range(count + 1)]
+    step = 2 if blk_parts == 1 else 1
+    count = min(CHUNKS, units)
+    cuts = [min(units, step * -(-units * c // (count * step))) for c in range(count + 1)]
     return inner, plane, row_parts, blk_parts, units, cuts
 
 
@@ -33,8 +35,9 @@
     return [tuple(range(b, min(b + 2, high))) for b in range(low, high, 2)]
 
 
-def kernel(n_chain, n_tok, q_ref, k_ref, v_ref, o_ref, xs, zs, qf, tot, got, plane_sum,
-           far_got, inc_send, inc, out_t, rs_send, rs_recv, z_send, z_recv, ag_send, ag_recv):
+def kernel(n_chain, n_tok, q_hbm, k_hbm, v_hbm, o_ref, q_ref, k_ref, v_ref, xs, zs, qf, tot, got,
+           plane_sum, far_got, inc_send, inc, out_t, in_sem, rs_send, rs_recv, z_send, z_recv,
+           ag_send, ag_recv):
     inner, plane, row_parts, blk_parts, units, cuts = layout(n_chain, n_tok)
     outer = n_chain // inner
     rows = WIDE // row_parts
@@ -43,6 +46,11 @@
     chain, tok = lax.axis_index("chain"), lax.axis_index("tok")
     z, me = chain // inner, (chain % inner) * n_tok + tok
 
+    loads = [pltpu.make_async_copy(src, dst, in_sem.at[i]) for i, (src, dst) in
+             enumerate(((k_hbm, k_ref), (v_hbm, v_ref), (q_hbm, q_ref)))]
+    for load in loads:
+        load.start()
+
     def in_plane(k):
         peer = (me + k) % plane
         return peer, (z * inner + peer // n_tok, peer % n_tok)
@@ -51,15 +59,15 @@
         return (((z + k) % outer) * inner + chain % inner, tok)
 
     barrier = pltpu.get_barrier_semaphore()
+    for k in range(1, outer):
+        pl.semaphore_signal(barrier, inc=1, device_id=along(k), device_id_type=MESH)
     for k in range(1, plane):
         pl.semaphore_signal(barrier, inc=1, device_id=in_plane(k)[1], device_id_type=MESH)
-    for k in range(1, outer):
-        pl.semaphore_signal(barrier, inc=1, device_id=along(k), device_id_type=MESH)
 
     root2 = math.sqrt(2.0)
 
     def prepare(ref):
-        @pl.loop(0, tiles)
+        @pl.loop(0, tiles, unroll=4)
         def _(t):
             x = ref[pl.ds(pl.multiple_of(t * LANES, LANES), LANES), :].astype(F32).T
             for h in range(HEADS):
@@ -122,8 +130,6 @@
     def span(c):
         return pl.ds(cuts[c], cuts[c + 1] - cuts[c])
 
-    started = []
-
     def scatter(c):
         for k in range(1, plane):
             peer, device = in_plane(k)
@@ -133,7 +139,6 @@
                 send_sem=rs_send.at[c, k], recv_sem=rs_recv.at[c, k],
                 device_id=device, device_id_type=MESH)
             copy.start()
-            started.append(copy)
             rs_copies[c].append(copy)
         blk, row = spot(c, me)
         got[0, span(c)] = tot[blk, row, :]
@@ -154,7 +159,6 @@
                 send_sem=z_send.at[c, k], recv_sem=z_recv.at[c, k],
                 device_id=along(k), device_id_type=MESH)
             copy.start()
-            started.append(copy)
             z_copies[c].append(copy)
 
     def gather(c):
@@ -174,7 +178,6 @@
                 send_sem=ag_send.at[c, k], recv_sem=ag_recv.at[c, k],
                 device_id=device, device_id_type=MESH)
             copy.start()
-            started.append(copy)
             ag_copies[c].append(copy)
         inc[blk, row, :] = inc_send[chain % inner, span(c)]
 
@@ -183,11 +186,10 @@
 
         @pl.loop(0, tiles)
         def _(t):
-            at = pl.ds(pl.multiple_of(t * LANES, LANES), LANES)
             for b in range(low, min(high, BLOCKS)):
                 for d in dists(b):
                     for h in range(HEADS):
-                        qf[h, pl.ds(d * HD, HD), at] = feats(h, t, d)
+                        qf[h, t, pl.ds(d * HD, HD), :] = feats(h, t, d)
 
     def read(c, first, last):
         for copy in ag_copies[c]:
@@ -205,8 +207,9 @@
                 for group in groups:
                     depth = sum(len(dists(b)) for b in group) * HD
                     state_t = joined([inc[b, row, :] for b in group])[:, :depth]
-                    more = jnp.dot(state_t, qf[h, pl.ds(group[0] * WIDE, depth), at],
-                                   preferred_element_type=F32)
+                    rhs = joined([qf[h, t, pl.ds(group[0] * WIDE, depth), :]
+                                  for t in range(k * DEEP // LANES, (k + 1) * DEEP // LANES)])
+                    more = jnp.dot(state_t, rhs, preferred_element_type=F32)
                     part = more if part is None else part + more
                 if last:
                     sums.append(part)
@@ -216,29 +219,34 @@
                 whole = jnp.concatenate(sums, axis=0)
                 for i in range(DEEP // LANES):
                     o_ref[pl.ds(k * DEEP + i * LANES, LANES), :] = (
-                        whole[:, i * LANES:(i + 1) * LANES].T * factor).astype(BF16)
+                        whole[:, i * LANES:(i + 1) * LANES].T * factor)
 
     n = len(cuts) - 1
     rs_copies, z_copies, ag_copies = ([[] for _ in range(n)] for _ in range(3))
 
+    loads[0].wait()
     prepare(k_ref)
-
+    loads[1].wait()
     for c in range(n):
         state(c)
         if c == 0:
             pl.semaphore_wait(barrier, plane - 1 + outer - 1)
         scatter(c)
-        if c >= 1:
-            spread(c - 1)
+    loads[2].wait()
     prepare(q_ref)
     for c in range(n):
+        spread(c)
         expand_queries(c)
-        if c == 0:
-            spread(n - 1)
-        gather(c)
-    for c in range(n):
-        read(c, c == 0, c == n - 1)
-    for copy in started:
+        if c == n - 1:
+            for e in range(n):
+                gather(e)
+    for c in range(n - 1):
+        read(c, c == 0, False)
+    for copies in rs_copies + z_copies + ag_copies[:-1]:
+        for copy in copies:
+            copy.wait_send()
+    read(n - 1, n == 1, True)
+    for copy in ag_copies[-1]:
         copy.wait_send()
 
 
@@ -248,15 +256,18 @@
     rows, tokens = WIDE // row_parts, queries.shape[0]
     blocks = units * blk_parts
     sems = pltpu.SemaphoreType.DMA
-    return pl.pallas_call(
+    out = pl.pallas_call(
         functools.partial(kernel, n_chain, n_tok),
-        out_shape=jax.ShapeDtypeStruct((tokens, WIDE), BF16),
-        in_specs=[pl.BlockSpec(memory_space=pltpu.VMEM)] * 3,
+        out_shape=pltpu.VMEM((tokens, WIDE), F32),
+        in_specs=[pl.BlockSpec(memory_space=pl.ANY)] * 3,
         out_specs=pl.BlockSpec(memory_space=pltpu.VMEM),
         scratch_shapes=[
+            pltpu.VMEM((tokens, WIDE), BF16),
+            pltpu.VMEM((tokens, WIDE), BF16),
+            pltpu.VMEM((tokens, WIDE), BF16),
             pltpu.VMEM((HEADS, tokens // LANES, HD, LANES), F32),
             pltpu.VMEM((HEADS, tokens // LANES, HD + HALF, LANES), F32),
-            pltpu.VMEM((HEADS, BLOCKS * WIDE, tokens), BF16),
+            pltpu.VMEM((HEADS, tokens // LANES, BLOCKS * WIDE, LANES), BF16),
             pltpu.VMEM((blocks, WIDE, WIDE), BF16),
             pltpu.VMEM((plane, units, rows, WIDE), BF16),
             pltpu.VMEM((units, rows, WIDE), BF16),
@@ -264,13 +275,15 @@
             pltpu.VMEM((inner, units, rows, WIDE), BF16),
             pltpu.VMEM((blocks, WIDE, WIDE), BF16),
             pltpu.VMEM((WIDE, tokens), F32),
+            sems((3,)),
             sems((n, plane)), sems((n, plane)),
             sems((n, max(outer, 1))), sems((n, max(outer, 1))),
             sems((n, plane)), sems((n, plane)),
         ],
         compiler_params=pltpu.CompilerParams(
-            collective_id=0, has_side_effects=True, vmem_limit_bytes=60 * 1024 * 1024),
+            collective_id=0, has_side_effects=True, vmem_limit_bytes=56 * 1024 * 1024),
     )(queries, keys, values)
+    return out.astype(BF16)
 
 
 def solution(mesh):

time: 30.4 us -> 26.4 us (0.87)
  Pallas kernels: 28.4 us -> 25.4 us
  local copies, waits for them, and re-layouts: 1.87 us -> 0 us
  other arithmetic: 0 us -> 0.85 us
    pallas_call x1, Pallas kernels: 28.4 us -> 25.4 us  [on_device(): pl.pallas_call(functools.partial(kernel, n_chain, n_tok), out_shape=pltpu...]
    unnamed x1 -> x0, local copies, waits for them, and re-layouts: 1.87 us -> none
    convert_element_type x0 -> x1, other arithmetic: none -> 0.85 us  [on_device(): return out.astype(BF16)]
where the time goes in v2:
time: 26.4 us; the launch traced here: 26.3 us
  Pallas kernels  25.4 us (96%)
  other arithmetic  0.85 us (3%)
    pallas_call x1, Pallas kernels, on_device(): pl.pallas_call(functools.partial(kernel, n_chain, n_tok), out_shape=pltpu...  25.4 us
    convert_element_type x1, other arithmetic, on_device(): return out.astype(BF16)  0.85 us

profile of v2, /device:TPU:0, one launch (start us, length us, event | category | flops | bytes accessed | tf_op | source)
XLA Modules:
  0.0 26.3 jit_solution(10618937064138100684)
XLA Ops:
  0.0 25.4 %shard_map.37 = f32[2048,128]{1,0:T(8,128)S(1)} custom-call(bf16[2048,128]{1,0:T(8,128)(2,1)} %q_hbm.1, bf16[2048,128]{1,0:T(8,128)(2,1)} %k_hbm.1, bf16[2048,128]{1,0:T(8,128)(2,1)} %v_hbm.1), custom_call_target="tpu_custom_call" | custom-call | tf_op jit(solution)/shard_map/pallas_call | solution.py:259
  25.4 0.8 %convert_element_type.3 = bf16[2048,128]{1,0:T(8,128)(2,1)} convert(f32[2048,128]{1,0:T(8,128)S(1)} %shard_map.37) | non-fusion elementwise | flops 262144 | bytes 1572864 | tf_op jit(solution)/shard_map/convert_element_type | solution.py:286

commit v3 on v2

--- a/solution.py
+++ b/solution.py
@@ -14,7 +14,8 @@
 HALF = HD // 2
 BLOCKS = HD // 4 + 1
 LANES, DEEP = 128, 256
-CHUNKS = 4
+CHUNKS = 9
+LAG_RELAY, LAG_SUM, LAG_READ, EARLY = 3, 4, 7, 3
 MESH = pl.DeviceIdType.MESH
 F32, BF16 = jnp.float32, jnp.bfloat16
 
@@ -36,7 +37,7 @@
 
 
 def kernel(n_chain, n_tok, q_hbm, k_hbm, v_hbm, o_ref, q_ref, k_ref, v_ref, xs, zs, qf, tot, got,
-           plane_sum, far_got, inc_send, inc, out_t, in_sem, rs_send, rs_recv, z_send, z_recv,
+           plane_sum, below, z_out, far_got, inc_send, inc, out_t, in_sem, rs_send, rs_recv, z_send, z_recv,
            ag_send, ag_recv):
     inner, plane, row_parts, blk_parts, units, cuts = layout(n_chain, n_tok)
     outer = n_chain // inner
@@ -45,22 +46,41 @@
     tiles = tokens // LANES
     chain, tok = lax.axis_index("chain"), lax.axis_index("tok")
     z, me = chain // inner, (chain % inner) * n_tok + tok
+    bits = [1 << i for i in range(plane.bit_length() - 1)] if plane & (plane - 1) == 0 else []
 
     loads = [pltpu.make_async_copy(src, dst, in_sem.at[i]) for i, (src, dst) in
              enumerate(((k_hbm, k_ref), (v_hbm, v_ref), (q_hbm, q_ref)))]
     for load in loads:
         load.start()
 
+    def other(k):
+        return (me + k - 2 * sum(me // p % 2 * p for p in bits if k & p)) if bits else (me + k) % plane
+
     def in_plane(k):
-        peer = (me + k) % plane
+        peer = other(k)
         return peer, (z * inner + peer // n_tok, peer % n_tok)
 
-    def along(k):
-        return (((z + k) % outer) * inner + chain % inner, tok)
+    def along(target):
+        return (target * inner + chain % inner, tok)
+
+    steps = (outer - 1).bit_length()
+
+    def takes(s):
+        return z // (1 << s) % 2 == 1
+
+    def gives(s):
+        return z % (2 << s) == (1 << s) - 1
 
     barrier = pltpu.get_barrier_semaphore()
-    for k in range(1, outer):
-        pl.semaphore_signal(barrier, inc=1, device_id=along(k), device_id_type=MESH)
+    greeted = plane - 1
+    for s in range(steps):
+        greeted = greeted + jnp.where(gives(s), 1 << s, 0)
+
+        @pl.when(takes(s))
+        def _():
+            pl.semaphore_signal(barrier, inc=1, device_id=along(z // (2 << s) * (2 << s) + (1 << s) - 1),
+                                device_id_type=MESH)
+
     for k in range(1, plane):
         pl.semaphore_signal(barrier, inc=1, device_id=in_plane(k)[1], device_id_type=MESH)
 
@@ -116,16 +136,22 @@
             if short:
                 both = jnp.concatenate([both, jnp.zeros((short, WIDE), F32)], axis=0)
             for i, b in enumerate(group):
-                tot[b] = both[i * WIDE:(i + 1) * WIDE].T.astype(BF16)
+                turned = both[i * WIDE:(i + 1) * WIDE].T.astype(BF16)
+                for r in range(row_parts):
+                    tot[r, b] = turned[r * rows:(r + 1) * rows]
         if high > max(low, real):
             first = max(low, real)
-            tot[pl.ds(first, high - first)] = jnp.zeros((high - first, WIDE, WIDE), BF16)
+            tot[:, pl.ds(first, high - first)] = jnp.zeros((row_parts, high - first, rows, WIDE), BF16)
+
+    def settle(ref, count, c, sem):
+        if count > 1:
+            some = ref.at[pl.ds(1, count - 1), span(c)]
+            pltpu.make_async_copy(some, some, sem.at[c]).wait()
 
     def spot(c, who):
         low, _ = blocks_of(c)
         size = cuts[c + 1] - cuts[c]
-        row = pl.multiple_of((who % row_parts) * rows, rows)
-        return pl.ds(low + (who // row_parts) * size, size), pl.ds(row, rows)
+        return who % row_parts, pl.ds(low + (who // row_parts) * size, size)
 
     def span(c):
         return pl.ds(cuts[c], cuts[c + 1] - cuts[c])
@@ -133,53 +159,73 @@
     def scatter(c):
         for k in range(1, plane):
             peer, device = in_plane(k)
-            blk, row = spot(c, peer)
+            part, blk = spot(c, peer)
             copy = pltpu.make_async_remote_copy(
-                src_ref=tot.at[blk, row, :], dst_ref=got.at[k, span(c)],
-                send_sem=rs_send.at[c, k], recv_sem=rs_recv.at[c, k],
+                src_ref=tot.at[part, blk], dst_ref=got.at[k, span(c)],
+                send_sem=rs_send.at[c], recv_sem=rs_recv.at[c],
                 device_id=device, device_id_type=MESH)
             copy.start()
-            rs_copies[c].append(copy)
-        blk, row = spot(c, me)
-        got[0, span(c)] = tot[blk, row, :]
+        part, blk = spot(c, me)
+        got[0, span(c)] = tot[part, blk]
 
     def piece(c, source):
-        return got[(me + plane - source) % plane, span(c)].astype(F32)
+        slot = other(source) if bits else (me + plane - source) % plane
+        return got[slot, span(c)].astype(F32)
 
     def spread(c):
-        for copy in rs_copies[c]:
-            copy.wait_recv()
+        settle(got, plane, c, rs_recv)
         total = piece(c, 0)
         for source in range(1, plane):
             total = total + piece(c, source)
-        plane_sum[span(c)] = total.astype(BF16)
-        for k in range(1, outer):
-            copy = pltpu.make_async_remote_copy(
-                src_ref=plane_sum.at[span(c)], dst_ref=far_got.at[k, span(c)],
-                send_sem=z_send.at[c, k], recv_sem=z_recv.at[c, k],
-                device_id=along(k), device_id_type=MESH)
-            copy.start()
-            z_copies[c].append(copy)
+        plane_sum[span(c)] = total
+        below[span(c)] = jnp.zeros((cuts[c + 1] - cuts[c], rows, WIDE), F32)
+        if steps:
+            give(c, 0)
+
+    def give(c, s):
+        @pl.when(gives(s))
+        def _():
+            z_out[s, span(c)] = (plane_sum[span(c)] + below[span(c)]).astype(BF16)
+            for k in range(1, (1 << s) + 1):
+                pltpu.make_async_remote_copy(
+                    src_ref=z_out.at[s, span(c)], dst_ref=far_got.at[s, span(c)],
+                    send_sem=z_send.at[s, c], recv_sem=z_recv.at[s, c],
+                    device_id=along(z + k), device_id_type=MESH).start()
+
+    def take(c, s):
+        @pl.when(takes(s))
+        def _():
+            some = far_got.at[s, span(c)]
+            pltpu.make_async_copy(some, some, z_recv.at[s, c]).wait()
+            below[span(c)] = below[span(c)] + far_got[s, span(c)].astype(F32)
+
+    def relay(c, s):
+        take(c, s - 1)
+        give(c, s)
+
+    def given(c, s):
+        @pl.when(gives(s))
+        def _():
+            some = got.at[pl.ds(0, 1 << s), span(c)]
+            pltpu.make_async_copy(some, some, z_send.at[s, c]).wait()
 
     def gather(c):
-        running = jnp.zeros((cuts[c + 1] - cuts[c], rows, WIDE), F32)
-        for k in range(1, outer):
-            z_copies[c][k - 1].wait_recv()
-            running = running + jnp.where(k <= z, far_got[k, span(c)].astype(F32), 0.0)
+        if steps:
+            take(c, steps - 1)
+        running = below[span(c)]
         for g in range(inner):
             for y in range(n_tok):
                 running = running + piece(c, g * n_tok + y)
             inc_send[g, span(c)] = running.astype(BF16)
-        blk, row = spot(c, me)
+        part, blk = spot(c, me)
         for k in range(1, plane):
             peer, device = in_plane(k)
             copy = pltpu.make_async_remote_copy(
-                src_ref=inc_send.at[peer // n_tok, span(c)], dst_ref=inc.at[blk, row, :],
-                send_sem=ag_send.at[c, k], recv_sem=ag_recv.at[c, k],
+                src_ref=inc_send.at[peer // n_tok, span(c)], dst_ref=inc.at[part, blk],
+                send_sem=ag_send.at[c], recv_sem=ag_recv.at[c],
                 device_id=device, device_id_type=MESH)
             copy.start()
-            ag_copies[c].append(copy)
-        inc[blk, row, :] = inc_send[chain % inner, span(c)]
+        inc[part, blk] = inc_send[chain % inner, span(c)]
 
     def expand_queries(c):
         low, high = blocks_of(c)
@@ -192,8 +238,7 @@
                         qf[h, t, pl.ds(d * HD, HD), :] = feats(h, t, d)
 
     def read(c, first, last):
-        for copy in ag_copies[c]:
-            copy.wait_recv()
+        settle(got, plane, c, ag_recv)
         low, high = blocks_of(c)
         groups = pairs(low, min(high, BLOCKS))
         count = (chain + 1).astype(F32) * (tokens * n_tok)
@@ -206,7 +251,8 @@
                 part = None if first else out_t[row, at]
                 for group in groups:
                     depth = sum(len(dists(b)) for b in group) * HD
-                    state_t = joined([inc[b, row, :] for b in group])[:, :depth]
+                    state_t = joined([joined([inc[r, b] for r in range(h * HD // rows, (h + 1) * HD // rows)],
+                                             axis=0) for b in group])[:, :depth]
                     rhs = joined([qf[h, t, pl.ds(group[0] * WIDE, depth), :]
                                   for t in range(k * DEEP // LANES, (k + 1) * DEEP // LANES)])
                     more = jnp.dot(state_t, rhs, preferred_element_type=F32)
@@ -222,39 +268,46 @@
                         whole[:, i * LANES:(i + 1) * LANES].T * factor)
 
     n = len(cuts) - 1
-    rs_copies, z_copies, ag_copies = ([[] for _ in range(n)] for _ in range(3))
-
+    early = min(EARLY, n - 1)
     loads[0].wait()
     prepare(k_ref)
     loads[1].wait()
     for c in range(n):
         state(c)
-        if c == 0:
-            pl.semaphore_wait(barrier, plane - 1 + outer - 1)
-        scatter(c)
+        if c == early:
+            pl.semaphore_wait(barrier, greeted)
+            for e in range(c):
+                scatter(e)
+        if c >= early:
+            scatter(c)
     loads[2].wait()
     prepare(q_ref)
-    for c in range(n):
-        spread(c)
-        expand_queries(c)
-        if c == n - 1:
-            for e in range(n):
-                gather(e)
-    for c in range(n - 1):
-        read(c, c == 0, False)
-    for copies in rs_copies + z_copies + ag_copies[:-1]:
-        for copy in copies:
-            copy.wait_send()
-    read(n - 1, n == 1, True)
-    for copy in ag_copies[-1]:
-        copy.wait_send()
+    summed = LAG_RELAY * max(steps - 1, 0) + LAG_SUM
+    for c in range(n + summed + LAG_READ):
+        if c < n:
+            spread(c)
+            expand_queries(c)
+        for s in range(1, steps):
+            if 0 <= c - LAG_RELAY * s < n:
+                relay(c - LAG_RELAY * s, s)
+        if 0 <= c - summed < n:
+            gather(c - summed)
+        done = c - summed - LAG_READ
+        if done == n - 1:
+            for i in range(n):
+                settle(got, plane, i, rs_send)
+                for s in range(steps):
+                    given(i, s)
+                settle(got, plane, i, ag_send)
+        if 0 <= done < n:
+            read(done, done == 0, done == n - 1)
 
 
 def on_device(n_chain, n_tok, queries, keys, values):
     inner, plane, row_parts, blk_parts, units, cuts = layout(n_chain, n_tok)
     outer, n = n_chain // inner, len(cuts) - 1
     rows, tokens = WIDE // row_parts, queries.shape[0]
-    blocks = units * blk_parts
+    blocks, steps = units * blk_parts, max((outer - 1).bit_length(), 1)
     sems = pltpu.SemaphoreType.DMA
     out = pl.pallas_call(
         functools.partial(kernel, n_chain, n_tok),
@@ -268,17 +321,17 @@
             pltpu.VMEM((HEADS, tokens // LANES, HD, LANES), F32),
             pltpu.VMEM((HEADS, tokens // LANES, HD + HALF, LANES), F32),
             pltpu.VMEM((HEADS, tokens // LANES, BLOCKS * WIDE, LANES), BF16),
-            pltpu.VMEM((blocks, WIDE, WIDE), BF16),
+            pltpu.VMEM((row_parts, blocks, rows, WIDE), BF16),
             pltpu.VMEM((plane, units, rows, WIDE), BF16),
-            pltpu.VMEM((units, rows, WIDE), BF16),
-            pltpu.VMEM((max(outer, 1), units, rows, WIDE), BF16),
+            pltpu.VMEM((units, rows, WIDE), F32),
+            pltpu.VMEM((units, rows, WIDE), F32),
+            pltpu.VMEM((steps, units, rows, WIDE), BF16),
+            pltpu.VMEM((steps, units, rows, WIDE), BF16),
             pltpu.VMEM((inner, units, rows, WIDE), BF16),
-            pltpu.VMEM((blocks, WIDE, WIDE), BF16),
+            pltpu.VMEM((row_parts, blocks, rows, WIDE), BF16),
             pltpu.VMEM((WIDE, tokens), F32),
             sems((3,)),
-            sems((n, plane)), sems((n, plane)),
-            sems((n, max(outer, 1))), sems((n, max(outer, 1))),
-            sems((n, plane)), sems((n, plane)),
+            sems((n,)), sems((n,)), sems((steps, n)), sems((steps, n)), sems((n,)), sems((n,)),
         ],
         compiler_params=pltpu.CompilerParams(
             collective_id=0, has_side_effects=True, vmem_limit_bytes=56 * 1024 * 1024),

time: 26.4 us -> 24.4 us (0.924)
  Pallas kernels: 25.4 us -> 23.4 us
    pallas_call x1, Pallas kernels: 25.4 us -> 23.4 us  [on_device(): pl.pallas_call(functools.partial(kernel, n_chain, n_tok), out_shape=pltpu...]
where the time goes in v3:
time: 24.4 us; the launch traced here: 24.3 us
  Pallas kernels  23.4 us (96%)
  other arithmetic  0.85 us (3%)
    pallas_call x1, Pallas kernels, on_device(): pl.pallas_call(functools.partial(kernel, n_chain, n_tok), out_shape=pltpu...  23.4 us
    convert_element_type x1, other arithmetic, on_device(): return out.astype(BF16)  0.85 us

profile of v3, /device:TPU:0, one launch (start us, length us, event | category | flops | bytes accessed | tf_op | source)
XLA Modules:
  0.0 24.3 jit_solution(5965474243229480655)
XLA Ops:
  0.0 23.4 %shard_map.37 = f32[2048,128]{1,0:T(8,128)S(1)} custom-call(bf16[2048,128]{1,0:T(8,128)(2,1)} %q_hbm.1, bf16[2048,128]{1,0:T(8,128)(2,1)} %k_hbm.1, bf16[2048,128]{1,0:T(8,128)(2,1)} %v_hbm.1), custom_call_target="tpu_custom_call" | custom-call | tf_op jit(solution)/shard_map/pallas_call | solution.py:312
  23.4 0.8 %convert_element_type.3 = bf16[2048,128]{1,0:T(8,128)(2,1)} convert(f32[2048,128]{1,0:T(8,128)S(1)} %shard_map.37) | non-fusion elementwise | flops 262144 | bytes 1572864 | tf_op jit(solution)/shard_map/convert_element_type | solution.py:339

commit v4 on v3

--- a/solution.py
+++ b/solution.py
@@ -15,7 +15,7 @@
 BLOCKS = HD // 4 + 1
 LANES, DEEP = 128, 256
 CHUNKS = 9
-LAG_RELAY, LAG_SUM, LAG_READ, EARLY = 3, 4, 7, 3
+LAG_RELAY, LAG_SUM, LAG_READ, EARLY = 2, 4, 7, 3
 MESH = pl.DeviceIdType.MESH
 F32, BF16 = jnp.float32, jnp.bfloat16
 

time: 24.4 us -> 24.1 us (0.988)
  Pallas kernels: 23.4 us -> 23.1 us
    pallas_call x1, Pallas kernels: 23.4 us -> 23.1 us  [on_device(): pl.pallas_call(functools.partial(kernel, n_chain, n_tok), out_shape=pltpu...]
where the time goes in v4:
time: 24.1 us; the launch traced here: 23.9 us
  Pallas kernels  23.1 us (96%)
  other arithmetic  0.85 us (4%)
    pallas_call x1, Pallas kernels, on_device(): pl.pallas_call(functools.partial(kernel, n_chain, n_tok), out_shape=pltpu...  23.1 us
    convert_element_type x1, other arithmetic, on_device(): return out.astype(BF16)  0.85 us

profile of v4, /device:TPU:0, one launch (start us, length us, event | category | flops | bytes accessed | tf_op | source)
XLA Modules:
  0.0 23.9 jit_solution(16314928085472461514)
XLA Ops:
  0.0 23.1 %shard_map.37 = f32[2048,128]{1,0:T(8,128)S(1)} custom-call(bf16[2048,128]{1,0:T(8,128)(2,1)} %q_hbm.1, bf16[2048,128]{1,0:T(8,128)(2,1)} %k_hbm.1, bf16[2048,128]{1,0:T(8,128)(2,1)} %v_hbm.1), custom_call_target="tpu_custom_call" | custom-call | tf_op jit(solution)/shard_map/pallas_call | solution.py:312
  23.1 0.8 %convert_element_type.3 = bf16[2048,128]{1,0:T(8,128)(2,1)} convert(f32[2048,128]{1,0:T(8,128)S(1)} %shard_map.37) | non-fusion elementwise | flops 262144 | bytes 1572864 | tf_op jit(solution)/shard_map/convert_element_type | solution.py:339

commit v5 on v4

--- a/solution.py
+++ b/solution.py
@@ -15,7 +15,7 @@
 BLOCKS = HD // 4 + 1
 LANES, DEEP = 128, 256
 CHUNKS = 9
-LAG_RELAY, LAG_SUM, LAG_READ, EARLY = 2, 4, 7, 3
+LAG_RELAY, LAG_SUM, LAG_READ, EARLY = 2, 4, 8, 3
 MESH = pl.DeviceIdType.MESH
 F32, BF16 = jnp.float32, jnp.bfloat16
 
@@ -29,6 +29,8 @@
     step = 2 if blk_parts == 1 else 1
     count = min(CHUNKS, units)
     cuts = [min(units, step * -(-units * c // (count * step))) for c in range(count + 1)]
+    if step == 2 and count > 2:
+        cuts = cuts[:1] + [c - 1 for c in cuts[1:-1]] + [units - 1, units]
     return inner, plane, row_parts, blk_parts, units, cuts
 
 
@@ -72,6 +74,8 @@
         return z % (2 << s) == (1 << s) - 1
 
     barrier = pltpu.get_barrier_semaphore()
+    for k in range(1, plane):
+        pl.semaphore_signal(barrier, inc=1, device_id=in_plane(k)[1], device_id_type=MESH)
     greeted = plane - 1
     for s in range(steps):
         greeted = greeted + jnp.where(gives(s), 1 << s, 0)
@@ -80,9 +84,6 @@
         def _():
             pl.semaphore_signal(barrier, inc=1, device_id=along(z // (2 << s) * (2 << s) + (1 << s) - 1),
                                 device_id_type=MESH)
-
-    for k in range(1, plane):
-        pl.semaphore_signal(barrier, inc=1, device_id=in_plane(k)[1], device_id_type=MESH)
 
     root2 = math.sqrt(2.0)
 
@@ -265,7 +266,7 @@
                 whole = jnp.concatenate(sums, axis=0)
                 for i in range(DEEP // LANES):
                     o_ref[pl.ds(k * DEEP + i * LANES, LANES), :] = (
-                        whole[:, i * LANES:(i + 1) * LANES].T * factor)
+                        whole[:, i * LANES:(i + 1) * LANES].T * factor).astype(BF16)
 
     n = len(cuts) - 1
     early = min(EARLY, n - 1)
@@ -281,11 +282,12 @@
         if c >= early:
             scatter(c)
     loads[2].wait()
-    prepare(q_ref)
     summed = LAG_RELAY * max(steps - 1, 0) + LAG_SUM
     for c in range(n + summed + LAG_READ):
         if c < n:
             spread(c)
+            if c == 0:
+                prepare(q_ref)
             expand_queries(c)
         for s in range(1, steps):
             if 0 <= c - LAG_RELAY * s < n:
@@ -311,7 +313,7 @@
     sems = pltpu.SemaphoreType.DMA
     out = pl.pallas_call(
         functools.partial(kernel, n_chain, n_tok),
-        out_shape=pltpu.VMEM((tokens, WIDE), F32),
+        out_shape=pltpu.VMEM((tokens, WIDE), BF16),
         in_specs=[pl.BlockSpec(memory_space=pl.ANY)] * 3,
         out_specs=pl.BlockSpec(memory_space=pltpu.VMEM),
         scratch_shapes=[
@@ -336,7 +338,7 @@
         compiler_params=pltpu.CompilerParams(
             collective_id=0, has_side_effects=True, vmem_limit_bytes=56 * 1024 * 1024),
     )(queries, keys, values)
-    return out.astype(BF16)
+    return out
 
 
 def solution(mesh):

time: 24.1 us -> 23.9 us (level)
  other arithmetic: 0.85 us -> 0 us
  local copies, waits for them, and re-layouts: 0 us -> 0.8 us
    convert_element_type x1 -> x0, other arithmetic: 0.85 us -> none  [on_device(): return out.astype(BF16)]
    unnamed x0 -> x1, local copies, waits for them, and re-layouts: none -> 0.8 us
where the time goes in v5:
time: 23.9 us; the launch traced here: 23.8 us
  Pallas kernels  23 us (96%)
  local copies, waits for them, and re-layouts  0.8 us (3%)
    pallas_call x1, Pallas kernels, on_device(): pl.pallas_call(functools.partial(kernel, n_chain, n_tok), out_shape=pltpu...  23 us
    unnamed x1, local copies, waits for them, and re-layouts  0.8 us

profile of v5, /device:TPU:0, one launch (start us, length us, event | category | flops | bytes accessed | tf_op | source)
XLA Modules:
  0.0 23.8 jit_solution(10366965728327919851)
XLA Ops:
  0.0 23.0 %shard_map.37 = bf16[2048,128]{1,0:T(8,128)(2,1)S(1)} custom-call(bf16[2048,128]{1,0:T(8,128)(2,1)} %q_hbm.1, bf16[2048,128]{1,0:T(8,128)(2,1)} %k_hbm.1, bf16[2048,128]{1,0:T(8,128)(2,1)} %v_hbm.1), custom_call_target="tpu_custom_call" | custom-call | tf_op jit(solution)/shard_map/pallas_call | solution.py:314
  23.0 0.8 %copy.5 = bf16[2048,128]{1,0:T(8,128)(2,1)} copy(bf16[2048,128]{1,0:T(8,128)(2,1)S(1)} %shard_map.37) | data formatting | bytes 1048576
